TPU v7x, 128 devices: a whole 4x4x4 slice. The times are simulated.
128 devices in a mesh: col: 16 (over y, z), row: 8 (over x, core).
Axes of the slice: x: 4, y: 4, z: 4, core: 2. Of those that a mesh axis runs over, the one named last changes fastest.
Arguments:
- u_factors: bfloat16 [2, 64, 256, 64, 128], P(None, 'row', None, 'col'), may hold values from -0.09375 to 0.09375
- v_factors: bfloat16 [2, 64, 256, 64, 128], P(None, 'row', None, 'col'), may hold values from -0.375 to 0.375
- ranks: int32 [2, 64, 64], P(None, 'row', 'col'), may hold values from 8 to 64
- model_init: float32 [2, 16384, 256], P(None, ('col', 'row')), may hold values from -6 to 6
- observed: float32 [2, 16384, 256], P(None, ('row', 'col')), may hold values from -6 to 6
- step: float32 [2], replicated, may hold values from 0.1 to 0.4
Outputs:
- model: float32 [2, 16384, 256], P(None, ('col', 'row'))
- misfit: float32 [2, 16384, 256], P(None, ('row', 'col'))
Inputs may be any that keep to these rules, and one draw needn't show every extreme that they name: `ranks`: columns of a factor beyond its tile's rank do not count.
All inputs are finite; a program needn't handle non-finite values.
Results may differ from a plain program's by a relative error of at most 0.0085.
Values may be sent and summed in bfloat16 or wider, within the bound.
A program may use at most 128 MiB of HBM per device.

v0:
```python
import jax
import jax.numpy as jnp
from jax import lax
from jax.sharding import PartitionSpec as P

ITERS = 2


def split_product(product, rank_mask, rank_most, right_count):
    real = product[..., :rank_most, :right_count] + product[..., rank_most:, right_count:]
    imaginary = product[..., :rank_most, right_count:] - product[..., rank_most:, :right_count]
    weights = rank_mask[..., None]
    return jnp.concatenate([real * weights, imaginary * weights], -1).astype(jnp.bfloat16)


def expand_complex(coefficient, right_count):
    real = coefficient[..., :right_count]
    imaginary = coefficient[..., right_count:]
    upper = jnp.concatenate([real, imaginary], -1)
    lower = jnp.concatenate([-imaginary, real], -1)
    return jnp.concatenate([upper, lower], -2)


def local(u_factors, v_factors, ranks, model_init, observed, step):
    frequencies = model_init.shape[0]
    rank_most = u_factors.shape[-1] // 2
    right_count = model_init.shape[-1] // 2
    tile_size = u_factors.shape[2]
    rows_here = u_factors.shape[1]
    cols_here = u_factors.shape[3]
    rank_mask = (
        jnp.arange(rank_most, dtype=jnp.int32)[None, None, None, :] < ranks[..., None]
    ).astype(jnp.float32)
    model = model_init
    misfit = model_init
    observed_block = lax.all_gather(observed, "col", axis=1, tiled=True)
    for sweep in range(ITERS):
        gathered = lax.all_gather(model.astype(jnp.bfloat16), "row", axis=1, tiled=True)
        model_tiles = gathered.reshape(frequencies, cols_here, tile_size, 2 * right_count)
        product = jnp.einsum(
            "fiajk,fjal->fijkl", v_factors, model_tiles, preferred_element_type=jnp.float32
        )
        coefficient = expand_complex(
            split_product(product, rank_mask, rank_most, right_count), right_count
        )
        partial_value = jnp.einsum(
            "fiajk,fijkl->fial", u_factors, coefficient, preferred_element_type=jnp.float32
        )
        partial_value = partial_value.reshape(frequencies, rows_here * tile_size, 2 * right_count)
        predicted = lax.psum(partial_value, "col")
        full_misfit = predicted - observed_block
        misfit_half = full_misfit.astype(jnp.bfloat16)
        share = observed.shape[1]
        misfit = lax.dynamic_slice_in_dim(full_misfit, lax.axis_index("col") * share, share, 1)
        misfit_tiles = misfit_half.reshape(frequencies, rows_here, tile_size, 2 * right_count)
        product = jnp.einsum(
            "fiajk,fial->fijkl", u_factors, misfit_tiles, preferred_element_type=jnp.float32
        )
        back = expand_complex(
            split_product(product, rank_mask, rank_most, right_count), right_count
        )
        gradient_part = jnp.einsum(
            "fiajk,fijkl->fjal", v_factors, back, preferred_element_type=jnp.float32
        )
        gradient_part = gradient_part.reshape(frequencies, cols_here * tile_size, 2 * right_count)
        gradient = lax.psum_scatter(gradient_part, "row", scatter_dimension=1, tiled=True)
        model = model - step[:, None, None] * gradient
    return (model, misfit)


def solution(mesh):
    return jax.shard_map(
        local,
        mesh=mesh,
        in_specs=(
            P(None, "row", None, "col", None),
            P(None, "row", None, "col", None),
            P(None, "row", "col"),
            P(None, ("col", "row"), None),
            P(None, ("row", "col"), None),
            P(),
        ),
        out_specs=(P(None, ("col", "row"), None), P(None, ("row", "col"), None)),
        check_vma=False,
    )
```

profile of v0, /device:TPU:0, one launch (start us, length us, event | category | flops | bytes accessed | tf_op | source)
XLA Modules:
  0.0 443.3 jit_solution(17294954381206863518)
XLA Ops:
  7.2 1.6 convert_element_type.23
  8.9 7.5 %copy.8 = bf16[2,8,256,4,128]{2,4,1,3,0:T(8,128)(2,1)} copy(bf16[2,8,256,4,128]{4,3,2,1,0:T(4,128)(2,1)} %param.7) | data formatting | bytes 8388608 | tf_op args[1]
  16.4 7.4 %copy.11 = bf16[2,8,256,4,128]{2,4,3,1,0:T(8,128)(2,1)} copy(bf16[2,8,256,4,128]{4,3,2,1,0:T(4,128)(2,1)} %param.6) | data formatting | bytes 8388608 | tf_op args[0]
  23.8 12.1 %all-gather.4.cloned.1.call-done = bf16[2,1024,256]{2,1,0:T(8,128)(2,1)} async-done(((bf16[2,128,256]{2,1,0:T(8,128)(2,1)}), bf16[2,1024,256]{2,1,0:T(8,128)(2,1)}) %all-gather.4.cloned.1.call-update) | async-done | bytes 1048592 | tf_op jit(solution)/shard_map/all_gather | solution.py:38
  36.0 3.7 fusion.49
  39.7 0.8 fusion.47
  41.2 1.5 copy-done
  42.7 2.9 fusion.18
  46.4 103.1 %all-reduce.3.cloned.1.call-done = f32[2,2048,256]{2,1,0:T(8,128)} async-done(((f32[2,2048,256]{2,1,0:T(8,128)}), f32[2,2048,256]{2,1,0:T(8,128)}) %all-reduce.3.cloned.1.call-update) | async-done | bytes 4194320 | tf_op jit(solution)/shard_map/psum | solution.py:50
  149.5 53.4 %all-gather.6.cloned.1.call-done = f32[2,2048,256]{2,1,0:T(8,128)} async-done(((f32[2,128,256]{2,1,0:T(8,128)}), f32[2,2048,256]{2,1,0:T(8,128)}) %all-gather.6.cloned.1.call-update) | async-done | bytes 4194320 | tf_op jit(solution)/shard_map/all_gather | solution.py:36
  202.9 4.3 subtract_convert_fusion
  207.5 1.3 fusion.50
  208.8 1.0 copy.31
  209.8 0.8 fusion.45
  211.3 1.5 copy-done.4
  212.8 2.8 fusion
  215.6 33.5 %reduce-scatter.3.cloned.1.call-done = f32[2,128,256]{2,1,0:T(8,128)} async-done(((f32[2,1024,256]{2,1,0:T(8,128)}), f32[2,128,256]{2,1,0:T(8,128)}) %reduce-scatter.3.cloned.1.call-update) | async-done | bytes 262160 | tf_op jit(solution)/shard_map/reduce_scatter | solution.py:66
  249.1 1.7 fusion.36
  250.9 22.4 %all-gather.8.cloned.1.call-done = bf16[2,1024,256]{2,1,0:T(8,128)(2,1)} async-done(((bf16[2,128,256]{2,1,0:T(8,128)(2,1)}), bf16[2,1024,256]{2,1,0:T(8,128)(2,1)}) %all-gather.8.cloned.1.call-update) | async-done | bytes 1048592 | tf_op jit(solution)/shard_map/all_gather | solution.py:38
  273.3 3.7 fusion.51
  278.6 1.5 copy-done.2
  280.0 2.9 fusion.16
  283.2 103.7 %all-reduce.5.cloned.1.call-done = f32[2,2048,256]{2,1,0:T(8,128)} async-done(((f32[2,2048,256]{2,1,0:T(8,128)}), f32[2,2048,256]{2,1,0:T(8,128)}) %all-reduce.5.cloned.1.call-update) | async-done | bytes 4194320 | tf_op jit(solution)/shard_map/psum | solution.py:50
  386.8 6.2 %fusion.42 = (bf16[2,2048,256]{2,1,0:T(8,128)(2,1)S(1)}, f32[2,2048,256]{2,1,0:T(8,128)}) fusion(f32[2,2048,256]{2,1,0:T(8,128)} %all-reduce.5.cloned.1.call-done, f32[2,2048,256]{2,1,0:T(8,128)} %all-gather.6.cloned.1.call-done), kind=kLoop, calls=%fused_computation.58 | loop fusion | flops 2097152 | bytes 14680064 | tf_op jit(solution)/shard_map/convert_element_type | solution.py:52
  393.0 1.3 fusion.52
  394.3 1.0 copy.30
  395.3 0.8 fusion.40
  396.8 1.5 copy-done.5
  398.3 2.8 fusion.8
  401.1 1.7 constant_dynamic-slice_fusion
  402.7 32.0 %reduce-scatter.5.cloned.1.call-done = f32[2,128,256]{2,1,0:T(8,128)} async-done(((f32[2,1024,256]{2,1,0:T(8,128)}), f32[2,128,256]{2,1,0:T(8,128)}) %reduce-scatter.5.cloned.1.call-update) | async-done | bytes 262160 | tf_op jit(solution)/shard_map/reduce_scatter | solution.py:66
  434.7 1.8 multiply_subtract_fusion
  (36 shorter events, 5.3 us)
Async XLA Ops:
  7.2 28.8 %all-gather.4.cloned.1.call-start = ((), (), s32[]{:S(2)}) async-start(), calls=%async_computation.2 | async-start | bytes 1179648 | tf_op jit(solution)/shard_map/all_gather | solution.py:38
  8.9 140.7 %all-reduce.3.cloned.1.call-start = ((), (), s32[]{:S(2)}) async-start(), calls=%async_computation.3 | async-start | bytes 8388608 | tf_op jit(solution)/shard_map/psum | solution.py:50
  16.4 7.4 %copy-start.8 = (s32[2,8,4]{1,2,0:T(4,128)S(1)}, s32[2,8,4]{1,2,0:T(4,128)}, u32[]{:S(2)}) copy-start(s32[2,8,4]{1,2,0:T(4,128)} %param.8) | copy-start | bytes 772
  40.5 2.2 copy-start
  45.6 157.3 %all-gather.6.cloned.1.call-start = ((), (), s32[]{:S(2)}) async-start(), calls=%async_computation.4 | async-start | bytes 4456448 | tf_op jit(solution)/shard_map/all_gather | solution.py:36
  46.4 202.7 %reduce-scatter.3.cloned.1.call-start = ((), (), s32[]{:S(2)}) async-start(), calls=%async_computation.5 | async-start | bytes 2359296 | tf_op jit(solution)/shard_map/reduce_scatter | solution.py:66
  202.9 4.6 %copy-start.1 = (bf16[2,8,256,4,128]{2,4,3,1,0:T(8,128)(2,1)S(1)}, bf16[2,8,256,4,128]{2,4,3,1,0:T(8,128)(2,1)}, u32[]{:S(2)}) copy-start(bf16[2,8,256,4,128]{2,4,3,1,0:T(8,128)(2,1)} %copy.11) | copy-start | bytes 12582916
  210.6 2.2 copy-start.4
  212.8 36.3 %copy-start.6 = (f32[2,128,256]{2,1,0:T(8,128)S(1)}, f32[2,128,256]{2,1,0:T(8,128)}, u32[]{:S(2)}) copy-start(f32[2,128,256]{2,1,0:T(8,128)} %param.9) | copy-start | bytes 786436
  212.8 36.3 %copy-start.9 = (f32[2]{0:T(128)S(1)}, f32[2]{0:T(128)}, u32[]{:S(2)}) copy-start(f32[2]{0:T(128)} %param.11) | copy-start | bytes 28
  215.6 57.7 %all-gather.8.cloned.1.call-start = ((), (), s32[]{:S(2)}) async-start(), calls=%async_computation.6 | async-start | bytes 1179648 | tf_op jit(solution)/shard_map/all_gather | solution.py:38
  250.8 136.0 %all-reduce.5.cloned.1.call-start = ((), (), s32[]{:S(2)}) async-start(), calls=%async_computation.7 | async-start | bytes 8388608 | tf_op jit(solution)/shard_map/psum | solution.py:50
  277.8 2.2 copy-start.2
  283.0 151.8 %reduce-scatter.5.cloned.1.call-start = ((), (), s32[]{:S(2)}) async-start(), calls=%async_computation.8 | async-start | bytes 2359296 | tf_op jit(solution)/shard_map/reduce_scatter | solution.py:66
  386.8 6.2 %copy-start.3 = (bf16[2,8,256,4,128]{2,4,3,1,0:T(8,128)(2,1)S(1)}, bf16[2,8,256,4,128]{2,4,3,1,0:T(8,128)(2,1)}, u32[]{:S(2)}) copy-start(bf16[2,8,256,4,128]{2,4,3,1,0:T(8,128)(2,1)} %copy.11) | copy-start | bytes 12582916
  396.1 2.2 copy-start.5
  398.3 36.5 %copy-start.7 = (f32[2,128,256]{2,1,0:T(8,128)S(1)}, f32[2,128,256]{2,1,0:T(8,128)}, u32[]{:S(2)}) copy-start(f32[2,128,256]{2,1,0:T(8,128)} %reduce-scatter.3.cloned.1.call-done) | copy-start | bytes 786436
Sparse Core Ops, SparseCore 0:
  10.2 25.6 all-gather.3
  45.7 103.7 all-reduce.2
  151.7 51.1 all-gather.5
  215.7 33.3 reduce-scatter.2
  251.2 22.0 all-gather.7
  283.1 103.7 all-reduce.4
  401.2 33.4 reduce-scatter.4
where the time goes:
time: 444 us; the launch traced here: 443 us
  waiting for transfers between devices  361 us (81%)
  local copies, waits for them, and re-layouts  24.7 us (6%)
  other arithmetic  21.6 us (5%)
  matrix products  21.4 us (5%)
  between operations  14.3 us (3%)
    psum x2, waiting for transfers between devices, local(): predicted = lax.psum(partial_value, 'col')  207 us
    reduce_scatter x2, waiting for transfers between devices, local(): lax.psum_scatter(gradient_part, 'row', scatter_dimension=1, tiled=True)  65.5 us
    all_gather x1, waiting for transfers between devices, local(): observed_block = lax.all_gather(observed, 'col', axis=1, tiled=True)  53.4 us
    all_gather x2, waiting for transfers between devices, local(): lax.all_gather(model.astype(jnp.bfloat16), 'row', axis=1, tiled=True)  34.6 us
    unnamed x22, local copies, waits for them, and re-layouts  21 us
    convert_element_type x2, other arithmetic, local(): misfit_half = full_misfit.astype(jnp.bfloat16)  10.5 us
    unnamed x4, matrix products  9.98 us
  transfers between devices with their start and end apart: 7, of which 7 were waited for; matrix products, arithmetic and copies ran while one was open for 4% of the time, Pallas kernels for 0%

commit v1 on v0

--- a/solution.py
+++ b/solution.py
@@ -47,7 +47,13 @@
             "fiajk,fijkl->fial", u_factors, coefficient, preferred_element_type=jnp.float32
         )
         partial_value = partial_value.reshape(frequencies, rows_here * tile_size, 2 * right_count)
-        predicted = lax.psum(partial_value, "col")
+        size = lax.axis_size("col")
+        predicted, hop = (partial_value, 1)
+        while hop < size:
+            predicted = predicted + lax.ppermute(
+                predicted, "col", [(i, i ^ hop) for i in range(size)]
+            )
+            hop = 2 * hop
         full_misfit = predicted - observed_block
         misfit_half = full_misfit.astype(jnp.bfloat16)
         share = observed.shape[1]

time: 444 us -> 958 us (2.16)
  waiting for transfers between devices: 361 us -> 841 us
  starting transfers between devices: 0.47 us -> 19.3 us
  other arithmetic: 21.6 us -> 35.3 us
    ppermute x0 -> x8, waiting for transfers between devices: none -> 741 us  [local(): lax.ppermute(predicted, 'col', [(i, i ^ hop) for i in range(size)])]
    psum x2 -> x0, waiting for transfers between devices: 207 us -> none  [local(): predicted = lax.psum(partial_value, 'col')]
    all_gather x1, waiting for transfers between devices: 53.4 us -> 0.01 us  [local(): observed_block = lax.all_gather(observed, 'col', axis=1, tiled=True)]
    ppermute x0 -> x8, starting transfers between devices: none -> 18.9 us  [local(): lax.ppermute(predicted, 'col', [(i, i ^ hop) for i in range(size)])]
    add x0 -> x6, other arithmetic: none -> 11.7 us  [local(): predicted + lax.ppermute(predicted, 'col', [(i, i ^ hop) for i in range(s...]
  transfers between devices with their start and end apart: 7 -> 13, of which waited for: 7 -> 12; matrix products, arithmetic and copies ran while one was open for 4% -> 2% of each run, Pallas kernels for 0% -> 0%
where the time goes in v1:
time: 958 us
  waiting for transfers between devices  841 us (88%)
  other arithmetic  35.3 us (4%)
  local copies, waits for them, and re-layouts  26.8 us (3%)
  matrix products  19.8 us (2%)
  starting transfers between devices  19.3 us (2%)
  between operations  15.4 us (2%)
    ppermute x8, waiting for transfers between devices, local(): lax.ppermute(predicted, 'col', [(i, i ^ hop) for i in range(size)])  741 us
    reduce_scatter x2, waiting for transfers between devices, local(): lax.psum_scatter(gradient_part, 'row', scatter_dimension=1, tiled=True)  66 us
    all_gather x2, waiting for transfers between devices, local(): lax.all_gather(model.astype(jnp.bfloat16), 'row', axis=1, tiled=True)  34.6 us
    unnamed x22, local copies, waits for them, and re-layouts  19.8 us
  transfers between devices with their start and end apart: 13, of which 12 were waited for; matrix products, arithmetic and copies ran while one was open for 2% of the time, Pallas kernels for 0%

profile of v1, /device:TPU:0, one launch (start us, length us, event | category | flops | bytes accessed | tf_op | source)
XLA Modules:
  0.0 957.8 jit_solution(15285363197640229625)
XLA Ops:
  9.7 7.5 copy.8
  17.2 7.3 copy.11
  24.6 12.2 %all-gather.4.cloned.1.call-done = bf16[2,1024,256]{2,1,0:T(8,128)(2,1)} async-done(((bf16[2,128,256]{2,1,0:T(8,128)(2,1)}), bf16[2,1024,256]{2,1,0:T(8,128)(2,1)}) %all-gather.4.cloned.1.call-update) | async-done | bytes 1048592 | tf_op jit(solution)/shard_map/all_gather | solution.py:38
  36.8 3.7 fusion.49
  43.5 2.1 fusion.18
  47.3 91.1 %collective-permute-done = f32[2,2048,256]{2,1,0:T(8,128)S(1)} collective-permute-done((f32[2,2048,256]{2,1,0:T(8,128)S(1)}, f32[2,2048,256]{2,1,0:T(8,128)S(1)}, u32[]{:S(2)}, u32[]{:S(2)}) %collective-permute-start) | collective-permute-done | bytes 4194336 | tf_op jit(solution)/shard_map/ppermute | solution.py:53
  139.5 3.2 collective-permute-start.1
  142.7 90.2 %collective-permute-done.1 = f32[2,2048,256]{2,1,0:T(8,128)S(1)} collective-permute-done((f32[2,2048,256]{2,1,0:T(8,128)S(1)}, f32[2,2048,256]{2,1,0:T(8,128)S(1)}, u32[]{:S(2)}, u32[]{:S(2)}) %collective-permute-start.1) | collective-permute-done | bytes 4194336 | tf_op jit(solution)/shard_map/ppermute | solution.py:53
  232.9 2.5 add.45
  237.0 110.8 %collective-permute-done.2 = f32[2,2048,256]{2,1,0:T(8,128)} collective-permute-done((f32[2,2048,256]{2,1,0:T(8,128)}, f32[2,2048,256]{2,1,0:T(8,128)}, u32[]{:S(2)}, u32[]{:S(2)}) %collective-permute-start.2) | collective-permute-done | bytes 4194336 | tf_op jit(solution)/shard_map/ppermute | solution.py:53
  347.8 6.0 add.46
  353.8 3.0 collective-permute-start.3
  356.8 88.9 %collective-permute-done.3 = f32[2,2048,256]{2,1,0:T(8,128)} collective-permute-done((f32[2,2048,256]{2,1,0:T(8,128)}, f32[2,2048,256]{2,1,0:T(8,128)}, u32[]{:S(2)}, u32[]{:S(2)}) %collective-permute-start.3) | collective-permute-done | bytes 4194336 | tf_op jit(solution)/shard_map/ppermute | solution.py:53
  445.7 5.5 subtract_convert_fusion
  456.5 2.8 fusion
  459.4 33.8 %reduce-scatter.3.cloned.1.call-done = f32[2,128,256]{2,1,0:T(8,128)} async-done(((f32[2,1024,256]{2,1,0:T(8,128)}), f32[2,128,256]{2,1,0:T(8,128)}) %reduce-scatter.3.cloned.1.call-update) | async-done | bytes 262160 | tf_op jit(solution)/shard_map/reduce_scatter | solution.py:72
  495.2 22.5 %all-gather.8.cloned.1.call-done = bf16[2,1024,256]{2,1,0:T(8,128)(2,1)} async-done(((bf16[2,128,256]{2,1,0:T(8,128)(2,1)}), bf16[2,1024,256]{2,1,0:T(8,128)(2,1)}) %all-gather.8.cloned.1.call-update) | async-done | bytes 1048592 | tf_op jit(solution)/shard_map/all_gather | solution.py:38
  517.6 3.7 fusion.51
  524.3 2.2 fusion.16
  528.2 91.1 %collective-permute-done.4 = f32[2,2048,256]{2,1,0:T(8,128)S(1)} collective-permute-done((f32[2,2048,256]{2,1,0:T(8,128)S(1)}, f32[2,2048,256]{2,1,0:T(8,128)S(1)}, u32[]{:S(2)}, u32[]{:S(2)}) %collective-permute-start.4) | collective-permute-done | bytes 4194336 | tf_op jit(solution)/shard_map/ppermute | solution.py:53
  620.4 3.2 collective-permute-start.5
  623.6 90.2 %collective-permute-done.5 = f32[2,2048,256]{2,1,0:T(8,128)S(1)} collective-permute-done((f32[2,2048,256]{2,1,0:T(8,128)S(1)}, f32[2,2048,256]{2,1,0:T(8,128)S(1)}, u32[]{:S(2)}, u32[]{:S(2)}) %collective-permute-start.5) | collective-permute-done | bytes 4194336 | tf_op jit(solution)/shard_map/ppermute | solution.py:53
  715.9 89.5 %collective-permute-done.6 = f32[2,2048,256]{2,1,0:T(8,128)S(1)} collective-permute-done((f32[2,2048,256]{2,1,0:T(8,128)S(1)}, f32[2,2048,256]{2,1,0:T(8,128)S(1)}, u32[]{:S(2)}, u32[]{:S(2)}) %collective-permute-start.6) | collective-permute-done | bytes 4194336 | tf_op jit(solution)/shard_map/ppermute | solution.py:53
  806.0 3.1 collective-permute-start.7
  809.1 88.6 %collective-permute-done.7 = f32[2,2048,256]{2,1,0:T(8,128)S(1)} collective-permute-done((f32[2,2048,256]{2,1,0:T(8,128)S(1)}, f32[2,2048,256]{2,1,0:T(8,128)S(1)}, u32[]{:S(2)}, u32[]{:S(2)}) %collective-permute-start.7) | collective-permute-done | bytes 4194336 | tf_op jit(solution)/shard_map/ppermute | solution.py:53
  897.7 2.9 fusion.42
  901.8 4.3 copy.30
  906.1 2.7 fusion.40
  908.7 2.8 fusion.23
  912.3 2.7 fusion.8
  916.7 32.2 %reduce-scatter.5.cloned.1.call-done = f32[2,128,256]{2,1,0:T(8,128)} async-done(((f32[2,1024,256]{2,1,0:T(8,128)}), f32[2,128,256]{2,1,0:T(8,128)}) %reduce-scatter.5.cloned.1.call-update) | async-done | bytes 262160 | tf_op jit(solution)/shard_map/reduce_scatter | solution.py:72
  948.9 1.8 multiply_subtract_fusion
  (52 shorter events, 28.2 us)
Async XLA Ops:
  8.0 28.8 %all-gather.4.cloned.1.call-start = ((), (), s32[]{:S(2)}) async-start(), calls=%async_computation.2 | async-start | bytes 1179648 | tf_op jit(solution)/shard_map/all_gather | solution.py:38
  9.7 347.1 %all-gather.6.cloned.1.call-start = ((), (), s32[]{:S(2)}) async-start(), calls=%async_computation.3 | async-start | bytes 4456448 | tf_op jit(solution)/shard_map/all_gather | solution.py:36
  17.2 7.3 copy-start.8
  41.3 2.2 copy-start
  45.7 92.8 %collective-permute-start = (f32[2,2048,256]{2,1,0:T(8,128)S(1)}, f32[2,2048,256]{2,1,0:T(8,128)S(1)}, u32[]{:S(2)}, u32[]{:S(2)}) collective-permute-start(f32[2,2048,256]{2,1,0:T(8,128)S(1)} %bitcast.79), channel_id=1, source_target_pairs={{0,8},{8,0},{16,24},{24,16},{32,40},{40,32},{48,56},{56,48},{64,72... | collective-permute-start | bytes 12582920 | tf_op jit(solution)/shard_map/ppermute | solution.py:53
  139.5 93.4 %collective-permute-start.1 = (f32[2,2048,256]{2,1,0:T(8,128)S(1)}, f32[2,2048,256]{2,1,0:T(8,128)S(1)}, u32[]{:S(2)}, u32[]{:S(2)}) collective-permute-start(f32[2,2048,256]{2,1,0:T(8,128)S(1)} %bitcast_add_fusion.1), channel_id=1, source_target_pairs={{0,16},{8,24},{16,0},{24,8},{32,48},{40,56},{48,32},{56,40},{64,80... | collective-permute-start | bytes 12582920 | tf_op jit(solution)/shard_map/ppermute | solution.py:53
  235.4 112.4 %collective-permute-start.2 = (f32[2,2048,256]{2,1,0:T(8,128)}, f32[2,2048,256]{2,1,0:T(8,128)}, u32[]{:S(2)}, u32[]{:S(2)}) collective-permute-start(f32[2,2048,256]{2,1,0:T(8,128)} %add.45), channel_id=1, source_target_pairs={{0,32},{8,40},{16,48},{24,56},{32,0},{40,8},{48,16},{56,24},{64,96... | collective-permute-start | bytes 12582920 | tf_op jit(solution)/shard_map/ppermute | solution.py:53
  237.0 256.2 %reduce-scatter.3.cloned.1.call-start = ((), (), s32[]{:S(2)}) async-start(), calls=%async_computation.4 | async-start | bytes 2359296 | tf_op jit(solution)/shard_map/reduce_scatter | solution.py:72
  353.8 91.9 %collective-permute-start.3 = (f32[2,2048,256]{2,1,0:T(8,128)}, f32[2,2048,256]{2,1,0:T(8,128)}, u32[]{:S(2)}, u32[]{:S(2)}) collective-permute-start(f32[2,2048,256]{2,1,0:T(8,128)} %add.46), channel_id=1, source_target_pairs={{0,64},{8,72},{16,80},{24,88},{32,96},{40,104},{48,112},{56,120},{... | collective-permute-start | bytes 12582920 | tf_op jit(solution)/shard_map/ppermute | solution.py:53
  356.8 94.5 %copy-start.1 = (bf16[2,8,256,4,128]{2,4,3,1,0:T(8,128)(2,1)S(1)}, bf16[2,8,256,4,128]{2,4,3,1,0:T(8,128)(2,1)}, u32[]{:S(2)}) copy-start(bf16[2,8,256,4,128]{2,4,3,1,0:T(8,128)(2,1)} %copy.11) | copy-start | bytes 12582916
  454.3 2.2 copy-start.3
  456.5 36.7 %copy-start.6 = (f32[2,128,256]{2,1,0:T(8,128)S(1)}, f32[2,128,256]{2,1,0:T(8,128)}, u32[]{:S(2)}) copy-start(f32[2,128,256]{2,1,0:T(8,128)} %param.9) | copy-start | bytes 786436
  456.5 36.7 %copy-start.9 = (f32[2]{0:T(128)S(1)}, f32[2]{0:T(128)}, u32[]{:S(2)}) copy-start(f32[2]{0:T(128)} %param.11) | copy-start | bytes 28
  459.3 58.3 %all-gather.8.cloned.1.call-start = ((), (), s32[]{:S(2)}) async-start(), calls=%async_computation.5 | async-start | bytes 1179648 | tf_op jit(solution)/shard_map/all_gather | solution.py:38
  494.9 453.9 %reduce-scatter.5.cloned.1.call-start = ((), (), s32[]{:S(2)}) async-start(), calls=%async_computation.6 | async-start | bytes 2359296 | tf_op jit(solution)/shard_map/reduce_scatter | solution.py:72
  522.1 2.2 copy-start.2
  526.5 92.8 %collective-permute-start.4 = (f32[2,2048,256]{2,1,0:T(8,128)S(1)}, f32[2,2048,256]{2,1,0:T(8,128)S(1)}, u32[]{:S(2)}, u32[]{:S(2)}) collective-permute-start(f32[2,2048,256]{2,1,0:T(8,128)S(1)} %bitcast.80), channel_id=1, source_target_pairs={{0,8},{8,0},{16,24},{24,16},{32,40},{40,32},{48,56},{56,48},{64,72... | collective-permute-start | bytes 12582920 | tf_op jit(solution)/shard_map/ppermute | solution.py:53
  620.4 93.4 %collective-permute-start.5 = (f32[2,2048,256]{2,1,0:T(8,128)S(1)}, f32[2,2048,256]{2,1,0:T(8,128)S(1)}, u32[]{:S(2)}, u32[]{:S(2)}) collective-permute-start(f32[2,2048,256]{2,1,0:T(8,128)S(1)} %bitcast_add_fusion), channel_id=1, source_target_pairs={{0,16},{8,24},{16,0},{24,8},{32,48},{40,56},{48,32},{56,40},{64,80... | collective-permute-start | bytes 12582920 | tf_op jit(solution)/shard_map/ppermute | solution.py:53
  714.3 183.3 %copy-start.5 = (f32[2,2048,256]{2,1,0:T(8,128)S(1)}, f32[2,2048,256]{2,1,0:T(8,128)}, u32[]{:S(2)}) copy-start(f32[2,2048,256]{2,1,0:T(8,128)} %all-gather.6.cloned.1.call-done) | copy-start | bytes 12582916
  714.4 91.1 %collective-permute-start.6 = (f32[2,2048,256]{2,1,0:T(8,128)S(1)}, f32[2,2048,256]{2,1,0:T(8,128)S(1)}, u32[]{:S(2)}, u32[]{:S(2)}) collective-permute-start(f32[2,2048,256]{2,1,0:T(8,128)S(1)} %add.51), channel_id=1, source_target_pairs={{0,32},{8,40},{16,48},{24,56},{32,0},{40,8},{48,16},{56,24},{64,96... | collective-permute-start | bytes 12582920 | tf_op jit(solution)/shard_map/ppermute | solution.py:53
  806.0 91.7 %collective-permute-start.7 = (f32[2,2048,256]{2,1,0:T(8,128)S(1)}, f32[2,2048,256]{2,1,0:T(8,128)S(1)}, u32[]{:S(2)}, u32[]{:S(2)}) collective-permute-start(f32[2,2048,256]{2,1,0:T(8,128)S(1)} %add.52), channel_id=1, source_target_pairs={{0,64},{8,72},{16,80},{24,88},{32,96},{40,104},{48,112},{56,120},{... | collective-permute-start | bytes 12582920 | tf_op jit(solution)/shard_map/ppermute | solution.py:53
  908.7 3.5 copy-start.4
  912.3 36.6 %copy-start.7 = (f32[2,128,256]{2,1,0:T(8,128)S(1)}, f32[2,128,256]{2,1,0:T(8,128)}, u32[]{:S(2)}) copy-start(f32[2,128,256]{2,1,0:T(8,128)} %reduce-scatter.3.cloned.1.call-done) | copy-start | bytes 786436
Sparse Core Ops, SparseCore 0:
  11.1 25.6 all-gather.3
  459.5 33.6 reduce-scatter.2
  495.5 22.1 all-gather.7
  915.1 33.6 reduce-scatter.4
Sparse Core Ops, SparseCore 1:
  237.0 67.7 all-gather.5
